TPU v7x, 512 devices: a whole 4x4x16 slice. The times are simulated.
512 devices in a mesh: utt: 8 (over y, z_hi), tm: 64 (over x, z_lo, core).
Axes of the slice: x: 4, y: 4, z: 16 (z_hi: 2, z_lo: 8; z = z_hi * 8 + z_lo), core: 2. Of those that a mesh axis runs over, the one named last changes fastest.
Arguments:
- stem: bfloat16 [65536, 1280], P(('utt', 'tm')), parts along dimension 0, may hold values from -8 to 8
- norm_gain: float32 [1280], replicated, may hold values from 0.25 to 1.75
- qkv_weight: bfloat16 [1280, 3840], P('tm'), may hold values from -0.2934839 to 0.2934839
- segment_ids: int32 [65536], P(('utt', 'tm')), parts along dimension 0, may hold values from 1 to 21, as said below
- dec_queries: bfloat16 [1024, 1280], P(('utt', 'tm')), parts along dimension 0, may hold values from -9 to 9
- stretch_mask: int32 [1024, 64], P(('utt', 'tm')), parts along dimension 0, may hold values 0 or 1
Outputs:
- memory: bfloat16 [65536, 1280], P(('utt', 'tm')), parts along dimension 0
- cross_out: bfloat16 [1024, 1280], P(('utt', 'tm')), parts along dimension 0
There are 8 independent parts, one for each index of `utt`. A program takes and returns all parts, laid end to end along the dimension named above; an argument that names none is the same for every part. Nothing has to cross between parts.
Inputs may be any that keep to these rules, and one draw needn't show every extreme that they name: `segment_ids`: ids start at 1 and rise by one from run to run; each id covers one contiguous run of at most 512 positions, and the last run is exactly 512 positions long.
All inputs are finite; a program needn't handle non-finite values. No bound on the sum of `stretch_mask` on one device may be relied on, other than what follows from the above.
Results may differ from a plain program's by a relative error of at most 0.0062.
Values may be sent and summed in bfloat16 or wider, within the bound.
A program may use at most 64 MiB of HBM per device.

v0:
```python
import math
import jax
import jax.numpy as jnp
from jax import lax
from jax.sharding import PartitionSpec as P

HD = 64


def from_behind(block, axis, distance):
    devices = range(lax.axis_size(axis))
    route = [(i - distance, i) for i in devices if i - distance in devices]
    return lax.ppermute(block, axis, route)


def on_device(stem, norm_gain, qkv_weight, segment_ids, dec_queries, stretch_mask):
    rows, width = stem.shape
    heads = width // HD
    scale = HD ** (-0.5)
    values_in = stem.astype(jnp.float32)
    mean = jnp.mean(values_in, axis=-1, keepdims=True)
    var = jnp.mean((values_in - mean) ** 2, axis=-1, keepdims=True)
    normed = ((values_in - mean) * lax.rsqrt(var + 1e-05) * norm_gain).astype(jnp.bfloat16)
    projected = jnp.dot(
        normed,
        lax.all_gather(qkv_weight, "tm", axis=0, tiled=True),
        preferred_element_type=jnp.float32,
    ).astype(jnp.bfloat16)
    query_part = projected[:, :width]
    keyvals = projected[:, width:]
    kv_pieces = []
    seg_pieces = []
    for offset in range(-4, 5):
        if offset == 0:
            kv_pieces.append(keyvals)
            seg_pieces.append(segment_ids)
        else:
            kv_pieces.append(from_behind(keyvals, "tm", -offset))
            seg_pieces.append(from_behind(segment_ids, "tm", -offset))
    extended = jnp.concatenate(kv_pieces, axis=0)
    seg_wide = jnp.concatenate(seg_pieces, axis=0)
    same = segment_ids[:, None] == seg_wide[None, :]
    group = math.gcd(heads, 4)
    span = group * HD
    groups = heads // group

    def attend(index):
        start = index * span
        query_group = lax.dynamic_slice_in_dim(query_part, start, span, 1).reshape(rows, group, HD)
        key_group = lax.dynamic_slice_in_dim(extended, start, span, 1).reshape(-1, group, HD)
        value_group = lax.dynamic_slice_in_dim(extended, width + start, span, 1).reshape(
            -1, group, HD
        )
        scores = (
            jnp.einsum("qhd,khd->hqk", query_group, key_group, preferred_element_type=jnp.float32)
            * scale
        )
        scores = jnp.where(same[None], scores, jnp.float32(-1e30))
        top = jnp.max(scores, axis=-1, keepdims=True)
        raised = jnp.exp(scores - top)
        probs = (raised / jnp.sum(raised, axis=-1, keepdims=True)).astype(jnp.bfloat16)
        context = jnp.einsum("hqk,khd->qhd", probs, value_group, preferred_element_type=jnp.float32)
        return context.reshape(rows, span)

    contexts = lax.map(attend, jnp.arange(groups, dtype=jnp.int32))
    context = jnp.transpose(contexts, (1, 0, 2)).reshape(rows, width)
    memory = (values_in + context).astype(jnp.bfloat16)
    tokens_dev = dec_queries.shape[0]
    all_queries = lax.all_gather(dec_queries, "tm", axis=0, tiled=True)
    all_masks = lax.all_gather(stretch_mask, "tm", axis=0, tiled=True)
    total_tokens = all_queries.shape[0]
    device = lax.axis_index("tm")
    column = lax.dynamic_slice_in_dim(all_masks, device, 1, 1)[:, 0]
    owner = jnp.arange(total_tokens, dtype=jnp.int32) // tokens_dev
    allowed = (column == 1) | (owner == device)
    query_heads = all_queries.reshape(total_tokens, heads, HD)
    memory_heads = memory.reshape(rows, heads, HD)
    cross = (
        jnp.einsum("thd,phd->htp", query_heads, memory_heads, preferred_element_type=jnp.float32)
        * scale
    )
    local_top = jnp.max(cross, axis=-1)
    weights = jnp.where(
        allowed[None, :, None], jnp.exp(cross - local_top[:, :, None]), jnp.float32(0.0)
    )
    denom = jnp.transpose(jnp.sum(weights, axis=-1))
    numer = jnp.einsum(
        "htp,phd->thd",
        weights.astype(jnp.bfloat16),
        memory_heads,
        preferred_element_type=jnp.float32,
    )
    top_masked = jnp.transpose(jnp.where(allowed[None, :], local_top, jnp.float32(-1e30)))
    num_all, top_all, den_all = (
        lax.all_to_all(numer[None], "tm", split_axis=1, concat_axis=0, tiled=True),
        lax.all_to_all(top_masked[None], "tm", split_axis=1, concat_axis=0, tiled=True),
        lax.all_to_all(denom[None], "tm", split_axis=1, concat_axis=0, tiled=True),
    )
    best = jnp.max(top_all, axis=0)
    factor = jnp.exp(top_all - best[None])
    num_total = jnp.sum(factor[..., None] * num_all, axis=0)
    den_total = jnp.sum(factor * den_all, axis=0)
    cross_out = (num_total / den_total[..., None]).reshape(tokens_dev, width).astype(jnp.bfloat16)
    return (memory, cross_out)


def solution(mesh):
    placed = (
        P(("utt", "tm"), None),
        P(),
        P("tm", None),
        P(("utt", "tm")),
        P(("utt", "tm"), None),
        P(("utt", "tm"), None),
    )
    return jax.shard_map(
        on_device,
        mesh=mesh,
        in_specs=placed,
        out_specs=(P(("utt", "tm"), None), P(("utt", "tm"), None)),
        check_vma=False,
    )
```

profile of v0, /device:TPU:1, one launch (start us, length us, event | category | flops | bytes accessed | tf_op | source)
XLA Modules:
  0.0 600.4 jit_solution(3820719611877599102)
XLA Ops:
  10.5 8.7 %collective-permute-start.12 = (s32[128]{0:T(128)}, s32[128]{0:T(128)S(1)}, u32[]{:S(2)}, u32[]{:S(2)}) collective-permute-start(s32[128]{0:T(128)} %param.11), channel_id=1, source_target_pairs={{1,0},{2,1},{3,2},{4,3},{5,4},{6,5},{7,6},{8,7},{9,8},{10,9},{11,1... | collective-permute-start | bytes 1544 | tf_op jit(solution)/shard_map/ppermute | solution.py:13
  19.3 4.2 collective-permute-start.11
  23.4 5.2 collective-permute-start.8
  28.6 116.4 %all-gather.1 = s32[64,2,64]{2,1,0:T(2,128)S(1)} all-gather(s32[1,2,64]{2,1,0:T(2,128)} %bitcast.74), channel_id=1, replica_groups=mesh['utt'=8,'tm'=64] {'tm'}, dimensions={0}, use_global_device_ids=true | all-gather | bytes 33280 | tf_op jit(solution)/shard_map/all_gather | solution.py:70
  146.7 114.0 %all-gather.2 = bf16[64,2,1280]{2,1,0:T(2,128)(2,1)S(1)} all-gather(bf16[1,2,1280]{2,1,0:T(2,128)(2,1)} %bitcast.73), channel_id=1, replica_groups=mesh['utt'=8,'tm'=64] {'tm'}, dimensions={0}, use_global_device_ids=true | all-gather | bytes 332800 | tf_op jit(solution)/shard_map/all_gather | solution.py:69
  263.4 6.1 %collective-permute-start.10 = (s32[128]{0:T(128)S(1)}, s32[128]{0:T(128)S(1)}, u32[]{:S(2)}, u32[]{:S(2)}) collective-permute-start(s32[128]{0:T(128)S(1)} %copy-done.1), channel_id=1, source_target_pairs={{0,2},{1,3},{2,4},{3,5},{4,6},{5,7},{6,8},{7,9},{8,10},{9,11},{10,... | collective-permute-start | bytes 1544 | tf_op jit(solution)/shard_map/ppermute | solution.py:13
  271.5 13.7 %reshape.128 = bf16[1280,3840]{1,0:T(8,128)(2,1)} reshape(bf16[64,20,3840]{2,1,0:T(8,128)(2,1)} %all-gather.5.cloned.1.call-done) | data formatting | bytes 19660800
  285.2 5.3 convolution_convert_fusion
  290.6 4.9 collective-permute-start
  295.6 5.5 collective-permute-start.1
  305.1 4.9 collective-permute-done
  310.0 24.2 %collective-permute-start.2 = (bf16[128,2560]{1,0:T(8,128)(2,1)S(1)}, bf16[128,2560]{1,0:T(8,128)(2,1)S(1)}, u32[]{:S(2)}, u32[]{:S(2)}) collective-permute-start(bf16[128,2560]{1,0:T(8,128)(2,1)S(1)} %slice.8), channel_id=1, source_target_pairs={{0,2},{1,3},{2,4},{3,5},{4,6},{5,7},{6,8},{7,9},{8,10},{9,11},{10,... | collective-permute-start | bytes 1966088 | tf_op jit(solution)/shard_map/ppermute | solution.py:13
  335.1 13.4 %collective-permute-start.3 = (bf16[128,2560]{1,0:T(8,128)(2,1)S(1)}, bf16[128,2560]{1,0:T(8,128)(2,1)S(1)}, u32[]{:S(2)}, u32[]{:S(2)}) collective-permute-start(bf16[128,2560]{1,0:T(8,128)(2,1)S(1)} %slice.8), channel_id=1, source_target_pairs={{0,1},{1,2},{2,3},{3,4},{4,5},{5,6},{6,7},{7,8},{8,9},{9,10},{10,1... | collective-permute-start | bytes 1966088 | tf_op jit(solution)/shard_map/ppermute | solution.py:13
  352.2 3.8 collective-permute-done.3
  357.9 53.3 %collective-permute-done.4 = bf16[128,2560]{1,0:T(8,128)(2,1)S(1)} collective-permute-done((bf16[128,2560]{1,0:T(8,128)(2,1)S(1)}, bf16[128,2560]{1,0:T(8,128)(2,1)S(1)}, u32[]{:S(2)}, u32[]{:S(2)}) %collective-permute-start.4) | collective-permute-done | bytes 655392 | tf_op jit(solution)/shard_map/ppermute | solution.py:13
  413.0 11.1 %collective-permute-done.6 = bf16[128,2560]{1,0:T(8,128)(2,1)S(1)} collective-permute-done((bf16[128,2560]{1,0:T(8,128)(2,1)S(1)}, bf16[128,2560]{1,0:T(8,128)(2,1)S(1)}, u32[]{:S(2)}, u32[]{:S(2)}) %collective-permute-start.6) | collective-permute-done | bytes 655392 | tf_op jit(solution)/shard_map/ppermute | solution.py:13
  425.9 8.9 %copy.40 = bf16[1152,2560]{0,1:T(8,128)(2,1)} copy(bf16[1152,2560]{1,0:T(8,128)(2,1)} %constant_dynamic-update-slice_fusion.1) | data formatting | bytes 11796480
  434.8 41.2 %while.13 = (s32[]{:T(128)}, f32[5,128,256]{1,2,0:T(8,128)}, s32[5]{0:T(128)S(1)}, bf16[1152,2560]{0,1:T(8,128)(2,1)}, bf16[128,1280]{1,0:T(8,128)(2,1)S(1)}, /*...) while((s32[]{:T(128)}, f32[5,128,256]{1,2,0:T(8,128)}, ...), condition=%wide.region_5.6_spmd.clone, body=%wide.region_2.5_spmd.clone.sunk | while | flops 154682496 | bytes 9282826 | solution.py:65
  437.7 2.4 fusion.45
  445.9 2.4 fusion.45
  448.3 2.3 fusion.46
  454.2 2.4 fusion.45
  462.4 2.4 fusion.45
  470.6 2.4 fusion.45
  478.7 32.9 %all-to-all-start.2 = ((f32[1,128,20]{2,0,1:T(1,128)}), f32[1,128,20]{2,0,1:T(1,128)S(1)}, u32[]{:S(2)}, u32[]{:S(2)}) async-start(f32[1,128,20]{2,0,1:T(1,128)} %copy.49), calls=%async_computation.2 | async-start | bytes 131072 | tf_op jit(solution)/shard_map/all_to_all | solution.py:97
  512.4 12.1 %all-to-all-done.2 = f32[1,128,20]{2,0,1:T(1,128)S(1)} async-done(((f32[1,128,20]{2,0,1:T(1,128)}), f32[1,128,20]{2,0,1:T(1,128)S(1)}, u32[]{:S(2)}, u32[]{:S(2)}) %all-to-all-start.2) | async-done | bytes 10272 | tf_op jit(solution)/shard_map/all_to_all | solution.py:97
  524.5 5.0 all-to-all-start
  530.7 2.5 copy.47
  533.7 3.9 reduce
  539.3 3.0 all-to-all-done
  542.3 10.1 %all-to-all-start.1 = ((f32[64,1,2560]{2,1,0:T(1,128)}), f32[64,1,2560]{2,1,0:T(1,128)S(1)}, u32[]{:S(2)}, u32[]{:S(2)}) async-start(f32[64,1,2560]{2,1,0:T(1,128)} %reshape.137), calls=%async_computation.1 | async-start | bytes 1310720 | tf_op jit(solution)/shard_map/all_to_all | solution.py:95
  554.3 32.7 %all-to-all-done.1 = f32[64,1,2560]{2,1,0:T(1,128)S(1)} async-done(((f32[64,1,2560]{2,1,0:T(1,128)}), f32[64,1,2560]{2,1,0:T(1,128)S(1)}, u32[]{:S(2)}, u32[]{:S(2)}) %all-to-all-start.1) | async-done | bytes 655392 | tf_op jit(solution)/shard_map/all_to_all | solution.py:95
  (117 shorter events, 62.4 us)
Async XLA Ops:
  7.2 254.2 %copy-start.1 = (s32[128]{0:T(128)S(1)}, s32[128]{0:T(128)}, u32[]{:S(2)}) copy-start(s32[128]{0:T(128)} %param.11) | copy-start | bytes 1540
  7.2 264.3 %all-gather.5.cloned.1.call-start = ((), (), s32[]{:S(2)}) async-start(), calls=%async_computation.3 | async-start | bytes 11980800 | tf_op jit(solution)/shard_map/all_gather | solution.py:26
  7.9 293.2 %collective-permute-start.14 = (s32[128]{0:T(128)}, s32[128]{0:T(128)S(1)}, u32[]{:S(2)}, u32[]{:S(2)}) collective-permute-start(s32[128]{0:T(128)} %param.11), channel_id=1, source_target_pairs={{3,0},{4,1},{5,2},{6,3},{7,4},{8,5},{9,6},{10,7},{11,8},{12,9},{13... | collective-permute-start | bytes 1544 | tf_op jit(solution)/shard_map/ppermute | solution.py:13
  9.2 291.9 %collective-permute-start.13 = (s32[128]{0:T(128)}, s32[128]{0:T(128)S(1)}, u32[]{:S(2)}, u32[]{:S(2)}) collective-permute-start(s32[128]{0:T(128)} %param.11), channel_id=1, source_target_pairs={{2,0},{3,1},{4,2},{5,3},{6,4},{7,5},{8,6},{9,7},{10,8},{11,9},{12,... | collective-permute-start | bytes 1544 | tf_op jit(solution)/shard_map/ppermute | solution.py:13
  10.5 285.0 %collective-permute-start.12 = (s32[128]{0:T(128)}, s32[128]{0:T(128)S(1)}, u32[]{:S(2)}, u32[]{:S(2)}) collective-permute-start(s32[128]{0:T(128)} %param.11), channel_id=1, source_target_pairs={{1,0},{2,1},{3,2},{4,3},{5,4},{6,5},{7,6},{8,7},{9,8},{10,9},{11,1... | collective-permute-start | bytes 1544 | tf_op jit(solution)/shard_map/ppermute | solution.py:13
  19.3 271.3 %collective-permute-start.11 = (s32[128]{0:T(128)}, s32[128]{0:T(128)S(1)}, u32[]{:S(2)}, u32[]{:S(2)}) collective-permute-start(s32[128]{0:T(128)} %param.11), channel_id=1, source_target_pairs={{0,1},{1,2},{2,3},{3,4},{4,5},{5,6},{6,7},{7,8},{8,9},{9,10},{10,1... | collective-permute-start | bytes 1544 | tf_op jit(solution)/shard_map/ppermute | solution.py:13
  23.4 237.9 %collective-permute-start.8 = (s32[128]{0:T(128)}, s32[128]{0:T(128)S(1)}, u32[]{:S(2)}, u32[]{:S(2)}) collective-permute-start(s32[128]{0:T(128)} %param.11), channel_id=1, source_target_pairs={{0,4},{1,5},{2,6},{3,7},{4,8},{5,9},{6,10},{7,11},{8,12},{9,13},{1... | collective-permute-start | bytes 1544 | tf_op jit(solution)/shard_map/ppermute | solution.py:13
  261.4 2.0 collective-permute-start.9
  263.4 6.8 %collective-permute-start.10 = (s32[128]{0:T(128)S(1)}, s32[128]{0:T(128)S(1)}, u32[]{:S(2)}, u32[]{:S(2)}) collective-permute-start(s32[128]{0:T(128)S(1)} %copy-done.1), channel_id=1, source_target_pairs={{0,2},{1,3},{2,4},{3,5},{4,6},{5,7},{6,8},{7,9},{8,10},{9,11},{10,... | collective-permute-start | bytes 1544 | tf_op jit(solution)/shard_map/ppermute | solution.py:13
  270.2 31.0 %collective-permute-start.15 = (s32[128]{0:T(128)S(1)}, s32[128]{0:T(128)S(1)}, u32[]{:S(2)}, u32[]{:S(2)}) collective-permute-start(s32[128]{0:T(128)S(1)} %copy-done.1), channel_id=1, source_target_pairs={{4,0},{5,1},{6,2},{7,3},{8,4},{9,5},{10,6},{11,7},{12,8},{13,9},{1... | collective-permute-start | bytes 1544 | tf_op jit(solution)/shard_map/ppermute | solution.py:13
  271.5 13.7 %copy-start.2 = (f32[1280]{0:T(1024)S(1)}, f32[1280]{0:T(1024)}, u32[]{:S(2)}) copy-start(f32[1280]{0:T(1024)} %param.9) | copy-start | bytes 15364
  290.5 66.5 %copy-start = (bf16[128,3840]{1,0:T(8,128)(2,1)}, bf16[128,3840]{1,0:T(8,128)(2,1)S(1)}, u32[]{:S(2)}) copy-start(bf16[128,3840]{1,0:T(8,128)(2,1)S(1)} %convolution_convert_fusion) | copy-start | bytes 2949124
  290.6 19.4 %collective-permute-start = (bf16[128,2560]{1,0:T(8,128)(2,1)S(1)}, bf16[128,2560]{1,0:T(8,128)(2,1)S(1)}, u32[]{:S(2)}, u32[]{:S(2)}) collective-permute-start(bf16[128,2560]{1,0:T(8,128)(2,1)S(1)} %slice.8), channel_id=1, source_target_pairs={{0,4},{1,5},{2,6},{3,7},{4,8},{5,9},{6,10},{7,11},{8,12},{9,13},{1... | collective-permute-start | bytes 1966088 | tf_op jit(solution)/shard_map/ppermute | solution.py:13
  295.6 39.6 %collective-permute-start.1 = (bf16[128,2560]{1,0:T(8,128)(2,1)S(1)}, bf16[128,2560]{1,0:T(8,128)(2,1)S(1)}, u32[]{:S(2)}, u32[]{:S(2)}) collective-permute-start(bf16[128,2560]{1,0:T(8,128)(2,1)S(1)} %slice.8), channel_id=1, source_target_pairs={{0,3},{1,4},{2,5},{3,6},{4,7},{5,8},{6,9},{7,10},{8,11},{9,12},{10... | collective-permute-start | bytes 1966088 | tf_op jit(solution)/shard_map/ppermute | solution.py:13
  301.2 123.8 %collective-permute-start.7 = (bf16[128,2560]{1,0:T(8,128)(2,1)S(1)}, bf16[128,2560]{1,0:T(8,128)(2,1)S(1)}, u32[]{:S(2)}, u32[]{:S(2)}) collective-permute-start(bf16[128,2560]{1,0:T(8,128)(2,1)S(1)} %slice.8), channel_id=1, source_target_pairs={{4,0},{5,1},{6,2},{7,3},{8,4},{9,5},{10,6},{11,7},{12,8},{13,9},{1... | collective-permute-start | bytes 1966088 | tf_op jit(solution)/shard_map/ppermute | solution.py:13
  302.5 121.6 %collective-permute-start.6 = (bf16[128,2560]{1,0:T(8,128)(2,1)S(1)}, bf16[128,2560]{1,0:T(8,128)(2,1)S(1)}, u32[]{:S(2)}, u32[]{:S(2)}) collective-permute-start(bf16[128,2560]{1,0:T(8,128)(2,1)S(1)} %slice.8), channel_id=1, source_target_pairs={{3,0},{4,1},{5,2},{6,3},{7,4},{8,5},{9,6},{10,7},{11,8},{12,9},{13... | collective-permute-start | bytes 1966088 | tf_op jit(solution)/shard_map/ppermute | solution.py:13
  303.8 108.4 %collective-permute-start.5 = (bf16[128,2560]{1,0:T(8,128)(2,1)S(1)}, bf16[128,2560]{1,0:T(8,128)(2,1)S(1)}, u32[]{:S(2)}, u32[]{:S(2)}) collective-permute-start(bf16[128,2560]{1,0:T(8,128)(2,1)S(1)} %slice.8), channel_id=1, source_target_pairs={{2,0},{3,1},{4,2},{5,3},{6,4},{7,5},{8,6},{9,7},{10,8},{11,9},{12,... | collective-permute-start | bytes 1966088 | tf_op jit(solution)/shard_map/ppermute | solution.py:13
  310.0 39.5 %collective-permute-start.2 = (bf16[128,2560]{1,0:T(8,128)(2,1)S(1)}, bf16[128,2560]{1,0:T(8,128)(2,1)S(1)}, u32[]{:S(2)}, u32[]{:S(2)}) collective-permute-start(bf16[128,2560]{1,0:T(8,128)(2,1)S(1)} %slice.8), channel_id=1, source_target_pairs={{0,2},{1,3},{2,4},{3,5},{4,6},{5,7},{6,8},{7,9},{8,10},{9,11},{10,... | collective-permute-start | bytes 1966088 | tf_op jit(solution)/shard_map/ppermute | solution.py:13
  335.1 20.9 %collective-permute-start.3 = (bf16[128,2560]{1,0:T(8,128)(2,1)S(1)}, bf16[128,2560]{1,0:T(8,128)(2,1)S(1)}, u32[]{:S(2)}, u32[]{:S(2)}) collective-permute-start(bf16[128,2560]{1,0:T(8,128)(2,1)S(1)} %slice.8), channel_id=1, source_target_pairs={{0,1},{1,2},{2,3},{3,4},{4,5},{5,6},{6,7},{7,8},{8,9},{9,10},{10,1... | collective-permute-start | bytes 1966088 | tf_op jit(solution)/shard_map/ppermute | solution.py:13
  349.5 61.8 %collective-permute-start.4 = (bf16[128,2560]{1,0:T(8,128)(2,1)S(1)}, bf16[128,2560]{1,0:T(8,128)(2,1)S(1)}, u32[]{:S(2)}, u32[]{:S(2)}) collective-permute-start(bf16[128,2560]{1,0:T(8,128)(2,1)S(1)} %slice.8), channel_id=1, source_target_pairs={{1,0},{2,1},{3,2},{4,3},{5,4},{6,5},{7,6},{8,7},{9,8},{10,9},{11,1... | collective-permute-start | bytes 1966088 | tf_op jit(solution)/shard_map/ppermute | solution.py:13
  425.9 8.9 %slice-start = ((bf16[128,3840]{1,0:T(8,128)(2,1)}), bf16[128,1280]{1,0:T(8,128)(2,1)S(1)}, s32[]{:S(2)}) async-start(bf16[128,3840]{1,0:T(8,128)(2,1)} %copy-done), calls=%async_computation.4 | async-start | bytes 655360 | tf_op jit(solution)/shard_map/slice | solution.py:29
  478.7 45.7 %all-to-all-start.2 = ((f32[1,128,20]{2,0,1:T(1,128)}), f32[1,128,20]{2,0,1:T(1,128)S(1)}, u32[]{:S(2)}, u32[]{:S(2)}) async-start(f32[1,128,20]{2,0,1:T(1,128)} %copy.49), calls=%async_computation.2 | async-start | bytes 131072 | tf_op jit(solution)/shard_map/all_to_all | solution.py:97
  524.5 17.8 %all-to-all-start = ((f32[1,128,20]{2,0,1:T(1,128)}), f32[1,128,20]{2,0,1:T(1,128)S(1)}, u32[]{:S(2)}, u32[]{:S(2)}) async-start(f32[1,128,20]{2,0,1:T(1,128)} %copy.44), calls=%async_computation | async-start | bytes 131072 | tf_op jit(solution)/shard_map/all_to_all | solution.py:96
  542.3 44.7 %all-to-all-start.1 = ((f32[64,1,2560]{2,1,0:T(1,128)}), f32[64,1,2560]{2,1,0:T(1,128)S(1)}, u32[]{:S(2)}, u32[]{:S(2)}) async-start(f32[64,1,2560]{2,1,0:T(1,128)} %reshape.137), calls=%async_computation.1 | async-start | bytes 1310720 | tf_op jit(solution)/shard_map/all_to_all | solution.py:95
Sparse Core Ops, SparseCore 0:
  10.1 136.0 all-gather.4
where the time goes:
time: 602 us; the launch traced here: 600 us
  blocking collectives  230 us (38%)
  starting transfers between devices  131 us (22%)
  waiting for transfers between devices  123 us (20%)
  local copies, waits for them, and re-layouts  56.6 us (9%)
  matrix products  30.5 us (5%)
  between operations  14.5 us (2%)
  other arithmetic  10.7 us (2%)
    all_gather x1, blocking collectives, on_device(): all_masks = lax.all_gather(stretch_mask, 'tm', axis=0, tiled=True)  116 us
    all_gather x1, blocking collectives, on_device(): all_queries = lax.all_gather(dec_queries, 'tm', axis=0, tiled=True)  114 us
    ppermute x16, starting transfers between devices, from_behind(): return lax.ppermute(block, axis, route)  83.2 us
    ppermute x16, waiting for transfers between devices, from_behind(): return lax.ppermute(block, axis, route)  74.5 us
    unnamed x30, local copies, waits for them, and re-layouts  35.9 us
    all_to_all x1, starting transfers between devices, on_device(): lax.all_to_all(denom[None], 'tm', split_axis=1, concat_axis=0, tiled=True)  32.9 us
    all_to_all x1, waiting for transfers between devices, on_device(): lax.all_to_all(numer[None], 'tm', split_axis=1, concat_axis=0, tiled=True)  32.7 us
    all_to_all x1, waiting for transfers between devices, on_device(): lax.all_to_all(denom[None], 'tm', split_axis=1, concat_axis=0, tiled=True)  12.1 us
  transfers between devices with their start and end apart: 20, of which 9 were waited for; matrix products, arithmetic and copies ran while one was open for 7% of the time, Pallas kernels for 0%

commit v1 on v0

--- a/solution.py
+++ b/solution.py
@@ -67,7 +67,9 @@
     memory = (values_in + context).astype(jnp.bfloat16)
     tokens_dev = dec_queries.shape[0]
     all_queries = lax.all_gather(dec_queries, "tm", axis=0, tiled=True)
-    all_masks = lax.all_gather(stretch_mask, "tm", axis=0, tiled=True)
+    all_masks = jnp.concatenate(
+        lax.all_to_all(jnp.stack([stretch_mask] * lax.axis_size("tm")), "tm", 0, 0), axis=0
+    )
     total_tokens = all_queries.shape[0]
     device = lax.axis_index("tm")
     column = lax.dynamic_slice_in_dim(all_masks, device, 1, 1)[:, 0]

time: 602 us -> 516 us (0.86)
  blocking collectives: 230 us -> 126 us
  starting transfers between devices: 131 us -> 147 us
    all_gather x1 -> x0, blocking collectives: 116 us -> none  [on_device(): all_masks = lax.all_gather(stretch_mask, 'tm', axis=0, tiled=True)]
    all_to_all x0 -> x1, starting transfers between devices: none -> 16.9 us  [on_device(): lax.all_to_all(jnp.stack([stretch_mask] * lax.axis_size('tm')), 'tm', 0, 0)]
    all_gather x1, blocking collectives: 114 us -> 126 us  [on_device(): all_queries = lax.all_gather(dec_queries, 'tm', axis=0, tiled=True)]
    unnamed x30 -> x31, local copies, waits for them, and re-layouts: 35.9 us -> 38.7 us
  transfers between devices with their start and end apart: 20 -> 21, of which waited for: 9 -> 8; matrix products, arithmetic and copies ran while one was open for 7% -> 9% of each run, Pallas kernels for 0% -> 0%
where the time goes in v1:
time: 516 us; the launch traced here: 514 us
  starting transfers between devices  147 us (28%)
  blocking collectives  126 us (24%)
  waiting for transfers between devices  119 us (23%)
  local copies, waits for them, and re-layouts  60.6 us (12%)
  matrix products  30.5 us (6%)
  between operations  14.5 us (3%)
  other arithmetic  11.5 us (2%)
    all_gather x1, blocking collectives, on_device(): all_queries = lax.all_gather(dec_queries, 'tm', axis=0, tiled=True)  126 us
    ppermute x16, starting transfers between devices, from_behind(): return lax.ppermute(block, axis, route)  83.5 us
    ppermute x16, waiting for transfers between devices, from_behind(): return lax.ppermute(block, axis, route)  70.8 us
    unnamed x31, local copies, waits for them, and re-layouts  38.7 us
    all_to_all x1, waiting for transfers between devices, on_device(): lax.all_to_all(numer[None], 'tm', split_axis=1, concat_axis=0, tiled=True)  32.7 us
    all_to_all x1, starting transfers between devices, on_device(): lax.all_to_all(denom[None], 'tm', split_axis=1, concat_axis=0, tiled=True)  31.9 us
    all_to_all x1, starting transfers between devices, on_device(): lax.all_to_all(jnp.stack([stretch_mask] * lax.axis_size('tm')), 'tm', 0, 0)  16.9 us
    all_to_all x1, waiting for transfers between devices, on_device(): lax.all_to_all(denom[None], 'tm', split_axis=1, concat_axis=0, tiled=True)  12.1 us
  transfers between devices with their start and end apart: 21, of which 8 were waited for; matrix products, arithmetic and copies ran while one was open for 9% of the time, Pallas kernels for 0%

profile of v1, /device:TPU:1, one launch (start us, length us, event | category | flops | bytes accessed | tf_op | source)
XLA Modules:
  0.0 513.6 jit_solution(3773944787560098799)
XLA Ops:
  10.5 8.7 %collective-permute-start.12 = (s32[128]{0:T(128)}, s32[128]{0:T(128)S(1)}, u32[]{:S(2)}, u32[]{:S(2)}) collective-permute-start(s32[128]{0:T(128)} %param.11), channel_id=1, source_target_pairs={{1,0},{2,1},{3,2},{4,3},{5,4},{6,5},{7,6},{8,7},{9,8},{10,9},{11,1... | collective-permute-start | bytes 1544 | tf_op jit(solution)/shard_map/ppermute | solution.py:13
  19.3 4.2 collective-permute-start.11
  23.4 5.2 %collective-permute-start.8 = (s32[128]{0:T(128)}, s32[128]{0:T(128)S(1)}, u32[]{:S(2)}, u32[]{:S(2)}) collective-permute-start(s32[128]{0:T(128)} %param.11), channel_id=1, source_target_pairs={{0,4},{1,5},{2,6},{3,7},{4,8},{5,9},{6,10},{7,11},{8,12},{9,13},{1... | collective-permute-start | bytes 1544 | tf_op jit(solution)/shard_map/ppermute | solution.py:13
  30.0 16.9 %all-to-all-start = ((s32[64,1,128]{2,1,0:T(1,128)}), s32[64,1,128]{2,1,0:T(1,128)S(1)}, u32[]{:S(2)}, u32[]{:S(2)}) async-start(s32[64,1,128]{2,1,0:T(1,128)} %reshape.142), calls=%async_computation | async-start | bytes 65536 | tf_op jit(solution)/shard_map/all_to_all | solution.py:71
  48.5 126.3 %all-gather.1 = bf16[64,2,1280]{2,1,0:T(2,128)(2,1)S(1)} all-gather(bf16[1,2,1280]{2,1,0:T(2,128)(2,1)} %bitcast.70), channel_id=1, replica_groups=mesh['utt'=8,'tm'=64] {'tm'}, dimensions={0}, use_global_device_ids=true | all-gather | bytes 332800 | tf_op jit(solution)/shard_map/all_gather | solution.py:69
  177.5 3.9 collective-permute-start.10
  183.5 13.7 %reshape.134 = bf16[1280,3840]{1,0:T(8,128)(2,1)} reshape(bf16[64,20,3840]{2,1,0:T(8,128)(2,1)} %all-gather.4.cloned.1.call-done) | data formatting | bytes 19660800
  197.2 5.3 %convolution_convert_fusion = bf16[128,3840]{1,0:T(8,128)(2,1)S(1)} fusion(bf16[1280,3840]{1,0:T(8,128)(2,1)} %reshape.134, bf16[128,1280]{0,1:T(8,128)(2,1)S(1)} %copy.46, f32[1280]{0:T(1024)S(1)} %copy-done.2, f32[128]{0:T(128)S(1)} %add_rsqrt_fusion, f32[128]{0:T(128)S(1)} %broadcast_multiply_fusion), kind=kOutput, calls=%fused_computation.16 | convolution fusion | flops 1259601920 | bytes 11147264 | tf_op jit(solution)/shard_map/dot_general | solution.py:24
  202.6 5.7 %collective-permute-start = (bf16[128,2560]{1,0:T(8,128)(2,1)S(1)}, bf16[128,2560]{1,0:T(8,128)(2,1)}, u32[]{:S(2)}, u32[]{:S(2)}) collective-permute-start(bf16[128,2560]{1,0:T(8,128)(2,1)S(1)} %slice.8), channel_id=1, source_target_pairs={{0,4},{1,5},{2,6},{3,7},{4,8},{5,9},{6,10},{7,11},{8,12},{9,13},{1... | collective-permute-start | bytes 1966088 | tf_op jit(solution)/shard_map/ppermute | solution.py:13
  208.4 7.7 %collective-permute-start.1 = (bf16[128,2560]{1,0:T(8,128)(2,1)S(1)}, bf16[128,2560]{1,0:T(8,128)(2,1)}, u32[]{:S(2)}, u32[]{:S(2)}) collective-permute-start(bf16[128,2560]{1,0:T(8,128)(2,1)S(1)} %slice.8), channel_id=1, source_target_pairs={{0,3},{1,4},{2,5},{3,6},{4,7},{5,8},{6,9},{7,10},{8,11},{9,12},{10... | collective-permute-start | bytes 1966088 | tf_op jit(solution)/shard_map/ppermute | solution.py:13
  221.5 24.6 %collective-permute-start.2 = (bf16[128,2560]{1,0:T(8,128)(2,1)S(1)}, bf16[128,2560]{1,0:T(8,128)(2,1)S(1)}, u32[]{:S(2)}, u32[]{:S(2)}) collective-permute-start(bf16[128,2560]{1,0:T(8,128)(2,1)S(1)} %slice.8), channel_id=1, source_target_pairs={{0,2},{1,3},{2,4},{3,5},{4,6},{5,7},{6,8},{7,9},{8,10},{9,11},{10,... | collective-permute-start | bytes 1966088 | tf_op jit(solution)/shard_map/ppermute | solution.py:13
  248.1 12.5 %collective-permute-start.3 = (bf16[128,2560]{1,0:T(8,128)(2,1)S(1)}, bf16[128,2560]{1,0:T(8,128)(2,1)S(1)}, u32[]{:S(2)}, u32[]{:S(2)}) collective-permute-start(bf16[128,2560]{1,0:T(8,128)(2,1)S(1)} %slice.8), channel_id=1, source_target_pairs={{0,1},{1,2},{2,3},{3,4},{4,5},{5,6},{6,7},{7,8},{8,9},{9,10},{10,1... | collective-permute-start | bytes 1966088 | tf_op jit(solution)/shard_map/ppermute | solution.py:13
  265.4 2.7 collective-permute-done.3
  270.0 54.6 %collective-permute-done.4 = bf16[128,2560]{1,0:T(8,128)(2,1)S(1)} collective-permute-done((bf16[128,2560]{1,0:T(8,128)(2,1)S(1)}, bf16[128,2560]{1,0:T(8,128)(2,1)S(1)}, u32[]{:S(2)}, u32[]{:S(2)}) %collective-permute-start.4) | collective-permute-done | bytes 655392 | tf_op jit(solution)/shard_map/ppermute | solution.py:13
  326.3 12.1 %collective-permute-done.6 = bf16[128,2560]{1,0:T(8,128)(2,1)S(1)} collective-permute-done((bf16[128,2560]{1,0:T(8,128)(2,1)S(1)}, bf16[128,2560]{1,0:T(8,128)(2,1)S(1)}, u32[]{:S(2)}, u32[]{:S(2)}) %collective-permute-start.6) | collective-permute-done | bytes 655392 | tf_op jit(solution)/shard_map/ppermute | solution.py:13
  340.2 8.9 %copy.47 = bf16[1152,2560]{0,1:T(8,128)(2,1)} copy(bf16[1152,2560]{1,0:T(8,128)(2,1)} %constant_dynamic-update-slice_fusion.1) | data formatting | bytes 11796480
  349.1 41.2 %while.13 = (s32[]{:T(128)}, f32[5,128,256]{1,2,0:T(8,128)}, s32[5]{0:T(128)S(1)}, bf16[1152,2560]{0,1:T(8,128)(2,1)}, bf16[128,1280]{1,0:T(8,128)(2,1)S(1)}, /*...) while((s32[]{:T(128)}, f32[5,128,256]{1,2,0:T(8,128)}, ...), condition=%wide.region_5.6_spmd.clone, body=%wide.region_2.5_spmd.clone.sunk | while | flops 154682496 | bytes 9282826 | solution.py:65
  352.0 2.4 fusion.46
  360.3 2.4 fusion.46
  362.6 2.3 fusion.47
  368.5 2.4 fusion.46
  376.8 2.4 fusion.46
  379.1 2.3 fusion.47
  385.0 2.4 fusion.46
  393.1 31.9 %all-to-all-start.3 = ((f32[1,128,20]{2,0,1:T(1,128)}), f32[1,128,20]{2,0,1:T(1,128)S(1)}, u32[]{:S(2)}, u32[]{:S(2)}) async-start(f32[1,128,20]{2,0,1:T(1,128)} %copy.55), calls=%async_computation.3 | async-start | bytes 131072 | tf_op jit(solution)/shard_map/all_to_all | solution.py:99
  425.7 12.1 %all-to-all-done.3 = f32[1,128,20]{2,0,1:T(1,128)S(1)} async-done(((f32[1,128,20]{2,0,1:T(1,128)}), f32[1,128,20]{2,0,1:T(1,128)S(1)}, u32[]{:S(2)}, u32[]{:S(2)}) %all-to-all-start.3) | async-done | bytes 10272 | tf_op jit(solution)/shard_map/all_to_all | solution.py:99
  437.8 5.0 all-to-all-start.1
  444.0 2.5 copy.53
  447.0 3.9 reduce.3
  452.6 3.0 all-to-all-done.1
  455.6 10.0 %all-to-all-start.2 = ((f32[64,1,2560]{2,1,0:T(1,128)}), f32[64,1,2560]{2,1,0:T(1,128)S(1)}, u32[]{:S(2)}, u32[]{:S(2)}) async-start(f32[64,1,2560]{2,1,0:T(1,128)} %reshape.144), calls=%async_computation.2 | async-start | bytes 1310720 | tf_op jit(solution)/shard_map/all_to_all | solution.py:97
  467.6 32.7 %all-to-all-done.2 = f32[64,1,2560]{2,1,0:T(1,128)S(1)} async-done(((f32[64,1,2560]{2,1,0:T(1,128)}), f32[64,1,2560]{2,1,0:T(1,128)S(1)}, u32[]{:S(2)}, u32[]{:S(2)}) %all-to-all-start.2) | async-done | bytes 655392 | tf_op jit(solution)/shard_map/all_to_all | solution.py:97
  (122 shorter events, 64.9 us)
Async XLA Ops:
  7.2 168.3 %copy-start.1 = (s32[128]{0:T(128)S(1)}, s32[128]{0:T(128)}, u32[]{:S(2)}) copy-start(s32[128]{0:T(128)} %param.11) | copy-start | bytes 1540
  7.2 176.3 %all-gather.4.cloned.1.call-start = ((), (), s32[]{:S(2)}) async-start(), calls=%async_computation.4 | async-start | bytes 11980800 | tf_op jit(solution)/shard_map/all_gather | solution.py:26
  7.9 200.4 %collective-permute-start.14 = (s32[128]{0:T(128)}, s32[128]{0:T(128)S(1)}, u32[]{:S(2)}, u32[]{:S(2)}) collective-permute-start(s32[128]{0:T(128)} %param.11), channel_id=1, source_target_pairs={{3,0},{4,1},{5,2},{6,3},{7,4},{8,5},{9,6},{10,7},{11,8},{12,9},{13... | collective-permute-start | bytes 1544 | tf_op jit(solution)/shard_map/ppermute | solution.py:13
  9.2 199.1 %collective-permute-start.13 = (s32[128]{0:T(128)}, s32[128]{0:T(128)S(1)}, u32[]{:S(2)}, u32[]{:S(2)}) collective-permute-start(s32[128]{0:T(128)} %param.11), channel_id=1, source_target_pairs={{2,0},{3,1},{4,2},{5,3},{6,4},{7,5},{8,6},{9,7},{10,8},{11,9},{12,... | collective-permute-start | bytes 1544 | tf_op jit(solution)/shard_map/ppermute | solution.py:13
  10.5 197.8 %collective-permute-start.12 = (s32[128]{0:T(128)}, s32[128]{0:T(128)S(1)}, u32[]{:S(2)}, u32[]{:S(2)}) collective-permute-start(s32[128]{0:T(128)} %param.11), channel_id=1, source_target_pairs={{1,0},{2,1},{3,2},{4,3},{5,4},{6,5},{7,6},{8,7},{9,8},{10,9},{11,1... | collective-permute-start | bytes 1544 | tf_op jit(solution)/shard_map/ppermute | solution.py:13
  19.3 164.1 %collective-permute-start.11 = (s32[128]{0:T(128)}, s32[128]{0:T(128)S(1)}, u32[]{:S(2)}, u32[]{:S(2)}) collective-permute-start(s32[128]{0:T(128)} %param.11), channel_id=1, source_target_pairs={{0,1},{1,2},{2,3},{3,4},{4,5},{5,6},{6,7},{7,8},{8,9},{9,10},{10,1... | collective-permute-start | bytes 1544 | tf_op jit(solution)/shard_map/ppermute | solution.py:13
  23.4 152.0 %collective-permute-start.8 = (s32[128]{0:T(128)}, s32[128]{0:T(128)S(1)}, u32[]{:S(2)}, u32[]{:S(2)}) collective-permute-start(s32[128]{0:T(128)} %param.11), channel_id=1, source_target_pairs={{0,4},{1,5},{2,6},{3,7},{4,8},{5,9},{6,10},{7,11},{8,12},{9,13},{1... | collective-permute-start | bytes 1544 | tf_op jit(solution)/shard_map/ppermute | solution.py:13
  30.0 186.0 %all-to-all-start = ((s32[64,1,128]{2,1,0:T(1,128)}), s32[64,1,128]{2,1,0:T(1,128)S(1)}, u32[]{:S(2)}, u32[]{:S(2)}) async-start(s32[64,1,128]{2,1,0:T(1,128)} %reshape.142), calls=%async_computation | async-start | bytes 65536 | tf_op jit(solution)/shard_map/all_to_all | solution.py:71
  175.5 2.0 collective-permute-start.9
  177.5 4.6 collective-permute-start.10
  182.1 33.9 %collective-permute-start.15 = (s32[128]{0:T(128)S(1)}, s32[128]{0:T(128)S(1)}, u32[]{:S(2)}, u32[]{:S(2)}) collective-permute-start(s32[128]{0:T(128)S(1)} %copy-done.1), channel_id=1, source_target_pairs={{4,0},{5,1},{6,2},{7,3},{8,4},{9,5},{10,6},{11,7},{12,8},{13,9},{1... | collective-permute-start | bytes 1544 | tf_op jit(solution)/shard_map/ppermute | solution.py:13
  183.4 13.7 %copy-start.2 = (f32[1280]{0:T(1024)S(1)}, f32[1280]{0:T(1024)}, u32[]{:S(2)}) copy-start(f32[1280]{0:T(1024)} %param.9) | copy-start | bytes 15364
  202.5 66.5 %copy-start = (bf16[128,3840]{1,0:T(8,128)(2,1)}, bf16[128,3840]{1,0:T(8,128)(2,1)S(1)}, u32[]{:S(2)}) copy-start(bf16[128,3840]{1,0:T(8,128)(2,1)S(1)} %convolution_convert_fusion) | copy-start | bytes 2949124
  202.6 18.9 %collective-permute-start = (bf16[128,2560]{1,0:T(8,128)(2,1)S(1)}, bf16[128,2560]{1,0:T(8,128)(2,1)}, u32[]{:S(2)}, u32[]{:S(2)}) collective-permute-start(bf16[128,2560]{1,0:T(8,128)(2,1)S(1)} %slice.8), channel_id=1, source_target_pairs={{0,4},{1,5},{2,6},{3,7},{4,8},{5,9},{6,10},{7,11},{8,12},{9,13},{1... | collective-permute-start | bytes 1966088 | tf_op jit(solution)/shard_map/ppermute | solution.py:13
  208.4 39.7 %collective-permute-start.1 = (bf16[128,2560]{1,0:T(8,128)(2,1)S(1)}, bf16[128,2560]{1,0:T(8,128)(2,1)}, u32[]{:S(2)}, u32[]{:S(2)}) collective-permute-start(bf16[128,2560]{1,0:T(8,128)(2,1)S(1)} %slice.8), channel_id=1, source_target_pairs={{0,3},{1,4},{2,5},{3,6},{4,7},{5,8},{6,9},{7,10},{8,11},{9,12},{10... | collective-permute-start | bytes 1966088 | tf_op jit(solution)/shard_map/ppermute | solution.py:13
  217.6 121.8 %collective-permute-start.7 = (bf16[128,2560]{1,0:T(8,128)(2,1)S(1)}, bf16[128,2560]{1,0:T(8,128)(2,1)S(1)}, u32[]{:S(2)}, u32[]{:S(2)}) collective-permute-start(bf16[128,2560]{1,0:T(8,128)(2,1)S(1)} %slice.8), channel_id=1, source_target_pairs={{4,0},{5,1},{6,2},{7,3},{8,4},{9,5},{10,6},{11,7},{12,8},{13,9},{1... | collective-permute-start | bytes 1966088 | tf_op jit(solution)/shard_map/ppermute | solution.py:13
  218.9 119.6 %collective-permute-start.6 = (bf16[128,2560]{1,0:T(8,128)(2,1)S(1)}, bf16[128,2560]{1,0:T(8,128)(2,1)S(1)}, u32[]{:S(2)}, u32[]{:S(2)}) collective-permute-start(bf16[128,2560]{1,0:T(8,128)(2,1)S(1)} %slice.8), channel_id=1, source_target_pairs={{3,0},{4,1},{5,2},{6,3},{7,4},{8,5},{9,6},{10,7},{11,8},{12,9},{13... | collective-permute-start | bytes 1966088 | tf_op jit(solution)/shard_map/ppermute | solution.py:13
  220.2 105.2 %collective-permute-start.5 = (bf16[128,2560]{1,0:T(8,128)(2,1)S(1)}, bf16[128,2560]{1,0:T(8,128)(2,1)S(1)}, u32[]{:S(2)}, u32[]{:S(2)}) collective-permute-start(bf16[128,2560]{1,0:T(8,128)(2,1)S(1)} %slice.8), channel_id=1, source_target_pairs={{2,0},{3,1},{4,2},{5,3},{6,4},{7,5},{8,6},{9,7},{10,8},{11,9},{12,... | collective-permute-start | bytes 1966088 | tf_op jit(solution)/shard_map/ppermute | solution.py:13
  221.5 41.1 %collective-permute-start.2 = (bf16[128,2560]{1,0:T(8,128)(2,1)S(1)}, bf16[128,2560]{1,0:T(8,128)(2,1)S(1)}, u32[]{:S(2)}, u32[]{:S(2)}) collective-permute-start(bf16[128,2560]{1,0:T(8,128)(2,1)S(1)} %slice.8), channel_id=1, source_target_pairs={{0,2},{1,3},{2,4},{3,5},{4,6},{5,7},{6,8},{7,9},{8,10},{9,11},{10,... | collective-permute-start | bytes 1966088 | tf_op jit(solution)/shard_map/ppermute | solution.py:13
  248.1 20.0 %collective-permute-start.3 = (bf16[128,2560]{1,0:T(8,128)(2,1)S(1)}, bf16[128,2560]{1,0:T(8,128)(2,1)S(1)}, u32[]{:S(2)}, u32[]{:S(2)}) collective-permute-start(bf16[128,2560]{1,0:T(8,128)(2,1)S(1)} %slice.8), channel_id=1, source_target_pairs={{0,1},{1,2},{2,3},{3,4},{4,5},{5,6},{6,7},{7,8},{8,9},{9,10},{10,1... | collective-permute-start | bytes 1966088 | tf_op jit(solution)/shard_map/ppermute | solution.py:13
  262.6 61.9 %collective-permute-start.4 = (bf16[128,2560]{1,0:T(8,128)(2,1)S(1)}, bf16[128,2560]{1,0:T(8,128)(2,1)S(1)}, u32[]{:S(2)}, u32[]{:S(2)}) collective-permute-start(bf16[128,2560]{1,0:T(8,128)(2,1)S(1)} %slice.8), channel_id=1, source_target_pairs={{1,0},{2,1},{3,2},{4,3},{5,4},{6,5},{7,6},{8,7},{9,8},{10,9},{11,1... | collective-permute-start | bytes 1966088 | tf_op jit(solution)/shard_map/ppermute | solution.py:13
  340.2 8.9 %slice-start = ((bf16[128,3840]{1,0:T(8,128)(2,1)}), bf16[128,1280]{1,0:T(8,128)(2,1)S(1)}, s32[]{:S(2)}) async-start(bf16[128,3840]{1,0:T(8,128)(2,1)} %copy-done), calls=%async_computation.5 | async-start | bytes 655360 | tf_op jit(solution)/shard_map/slice | solution.py:29
  393.1 44.7 %all-to-all-start.3 = ((f32[1,128,20]{2,0,1:T(1,128)}), f32[1,128,20]{2,0,1:T(1,128)S(1)}, u32[]{:S(2)}, u32[]{:S(2)}) async-start(f32[1,128,20]{2,0,1:T(1,128)} %copy.55), calls=%async_computation.3 | async-start | bytes 131072 | tf_op jit(solution)/shard_map/all_to_all | solution.py:99
  437.8 17.8 %all-to-all-start.1 = ((f32[1,128,20]{2,0,1:T(1,128)}), f32[1,128,20]{2,0,1:T(1,128)S(1)}, u32[]{:S(2)}, u32[]{:S(2)}) async-start(f32[1,128,20]{2,0,1:T(1,128)} %copy.50), calls=%async_computation.1 | async-start | bytes 131072 | tf_op jit(solution)/shard_map/all_to_all | solution.py:98
  455.6 44.7 %all-to-all-start.2 = ((f32[64,1,2560]{2,1,0:T(1,128)}), f32[64,1,2560]{2,1,0:T(1,128)S(1)}, u32[]{:S(2)}, u32[]{:S(2)}) async-start(f32[64,1,2560]{2,1,0:T(1,128)} %reshape.144), calls=%async_computation.2 | async-start | bytes 1310720 | tf_op jit(solution)/shard_map/all_to_all | solution.py:97
Sparse Core Ops, SparseCore 0:
  10.1 137.9 all-gather.3
